TPU v7x, 256 devices: a whole 4x4x8 slice. The times are simulated.
256 devices in a mesh: gx: 4 (over y), gy: 8 (over x, core), gz: 8 (over z).
Axes of the slice: x: 4, y: 4, z: 8, core: 2. Of those that a mesh axis runs over, the one named last changes fastest.
Arguments:
- measures: float32 [524288, 256], P(('gx', 'gy', 'gz')), may hold values from -6 to 6
- group_index: int32 [524288], P(('gx', 'gy', 'gz')), may hold values from 0 to 511, as said below
- distinct_keys: int32 [256, 512], P(('gx', 'gy', 'gz')), may hold values from 256 to 524543, as said below
- group_counts: int32 [256], P(('gx', 'gy', 'gz')), may hold values from 128 to 512, as said below
Outputs:
- group_sums: float32 [131072, 256], P(('gx', 'gy', 'gz'))
- group_rows: int32 [131072], P(('gx', 'gy', 'gz'))
- group_keys: int32 [131072], P(('gx', 'gy', 'gz'))
- group_total: int32 [], replicated
Inputs may be any that keep to these rules, and one draw needn't show every extreme that they name: `group_counts`: every device has between 128 and 512 groups, and some device has exactly 512. `group_index`: each row's index lies below its device's group count, and every group of a device has at least one row. `distinct_keys`: each device's keys rise strictly; all keys of device d equal d modulo 256, so no key lives on two devices; entries at and past the device's count are unused.
All inputs are finite; a program needn't handle non-finite values.
Results may differ from a plain program's by a relative error of at most 0.0003.
Values sent between devices are 32-bit elements; how exact they have to be, the bound alone decides.
A program may use at most 64 MiB of HBM per device.

v0:
```python
import jax
import jax.numpy as jnp
from jax import lax
from jax.sharding import Mesh
from jax.sharding import PartitionSpec as P

GX_GY_GZ = ("gx", "gy_0", "gy_1", "gz")
GY = ("gy_0", "gy_1")
GZ_GX_GY = ("gz", "gx", "gy_0", "gy_1")
GX_GY = ("gx", "gy_0", "gy_1")


def copy_for_each(x, axis):
    copies = jnp.broadcast_to(x, (lax.axis_size(axis), *x.shape))
    return lax.all_to_all(copies, axis, split_axis=0, concat_axis=0, tiled=True)


def joined_along(tiles, dim):
    dims = list(tiles.shape[1:])
    dims[dim] *= tiles.shape[0]
    return jnp.moveaxis(tiles, 0, dim).reshape(dims)


def whole_of(x, axes, dim):
    far, near = axes
    first = copy_for_each(x, far)
    tiles = jnp.swapaxes(copy_for_each(first, near), 0, 1)
    return joined_along(tiles.reshape(-1, *x.shape), dim)


def cut_along(x, dim, count):
    dims = x.shape
    tiles = x.reshape(*dims[:dim], count, dims[dim] // count, *dims[dim + 1 :])
    return jnp.moveaxis(tiles, dim, 0)


def one_exchange(x, axis, axes, splits, concats):
    sizes = [lax.axis_size(a) for a in axes]
    tiles = cut_along(x, splits[0], sizes[0])
    tiles = jnp.moveaxis(cut_along(tiles, splits[1] + 1, sizes[1]), 0, 1)
    inside = tiles.shape[2:]
    tiles = tiles.reshape(-1, *inside)
    tiles = lax.all_to_all(tiles, axis, split_axis=0, concat_axis=0, tiled=True)
    tiles = joined_along(tiles.reshape(*sizes, *inside), concats[0] + 1)
    return joined_along(tiles, concats[1])


def shards(measures, group_index, distinct_keys, group_counts):
    rows, width = measures.shape
    span = distinct_keys.shape[1]
    devices = lax.axis_size(GX_GY_GZ)
    slots = span // devices
    plane = lax.axis_size("gx") * lax.axis_size(GY)
    line = lax.axis_size("gz")
    count = group_counts[0]
    myself = jnp.int32(0)
    sender_counts = whole_of(group_counts, (("gx", "gy_0"), ("gy_1", "gz")), 0)
    sender_offsets = jnp.cumsum(sender_counts) - sender_counts
    myself = lax.axis_index(GX_GY_GZ)
    offset = sender_offsets[myself]
    group_total = jnp.sum(sender_counts)
    block = min(1024, rows)
    labels = lax.broadcasted_iota(jnp.int32, (span, block), 0)

    def accumulate(step, carry):
        totals, tallies = carry
        start = step * block
        index = lax.dynamic_slice_in_dim(group_index, start, block)
        values = lax.dynamic_slice_in_dim(measures, start, block, 0)
        hits = index[None, :] == labels
        totals = totals + jnp.dot(
            hits.astype(jnp.float32),
            values,
            precision=lax.Precision.HIGHEST,
            preferred_element_type=jnp.float32,
        )
        tallies = tallies + jnp.sum(hits, axis=1, dtype=jnp.int32)
        return (totals, tallies)

    sums, tallies = lax.fori_loop(
        0,
        rows // block,
        accumulate,
        (jnp.zeros((span, width), jnp.float32), jnp.zeros((span,), jnp.int32)),
    )
    local = jnp.arange(span, dtype=jnp.int32)
    live = local < count
    keys = jnp.where(live, distinct_keys[0], -1)
    fields = jnp.stack([tallies.astype(jnp.float32), keys.astype(jnp.float32)], axis=1)
    extra = fields.shape[1]
    array = jnp.concatenate([sums, fields], axis=1)
    shaped = array.reshape((slots, devices) + array.shape[1:])
    rolled = jnp.roll(shaped, offset, axis=1)
    outgoing = rolled.reshape((slots, plane, line) + array.shape[1:])
    arrived = one_exchange(outgoing, GZ_GX_GY, ("gz", GX_GY), (2, 1), (2, 1))
    got_sums = arrived[..., :width]
    got_fields = arrived[..., width:]
    got_fields = got_fields.reshape(-1, extra)
    sender = jnp.arange(devices, dtype=jnp.int32).reshape(1, plane, line)
    start_of = sender_offsets.reshape(1, plane, line)
    count_of = sender_counts.reshape(1, plane, line)
    level = jnp.arange(slots, dtype=jnp.int32).reshape(slots, 1, 1)
    position = level * devices + (myself - start_of) % devices
    arrived_live = (position < count_of) & (sender >= 0)
    target = jnp.where(arrived_live, (start_of + position) // devices, span).reshape(-1)
    group_sums = (
        jnp.zeros((span, width), jnp.float32)
        .at[target]
        .set(got_sums.reshape(-1, width), mode="drop")
    )
    group_rows = (
        jnp.zeros((span,), jnp.int32)
        .at[target]
        .set(got_fields[:, 0].astype(jnp.int32), mode="drop")
    )
    group_keys = (
        jnp.full((span,), -1, jnp.int32)
        .at[target]
        .set(got_fields[:, 1].astype(jnp.int32), mode="drop")
    )
    return (group_sums, group_rows, group_keys, group_total)


def solution(mesh):
    finer = Mesh(
        mesh.devices.reshape(mesh.shape["gx"], 4, 2, mesh.shape["gz"]), ("gx", "gy_0", "gy_1", "gz")
    )
    in_specs = (P(GX_GY_GZ, None), P(GX_GY_GZ), P(GX_GY_GZ, None), P(GX_GY_GZ))
    out_specs = (P(GX_GY_GZ, None), P(GX_GY_GZ), P(GX_GY_GZ), P())
    return jax.shard_map(
        shards, mesh=finer, in_specs=in_specs, out_specs=out_specs, check_vma=False
    )
```

profile of v0, /device:TPU:1, one launch (start us, length us, event | category | flops | bytes accessed | tf_op | source)
XLA Modules:
  0.0 85.1 jit_solution(16227952208858228809)
XLA Ops:
  1.3 0.6 broadcast_in_dim.23
  1.9 7.6 %all-to-all-start = ((s32[16,1,1]{2,1,0:T(1,128)}), s32[16,1,1]{2,1,0:T(1,128)S(1)}, u32[]{:S(2)}, u32[]{:S(2)}) async-start(s32[16,1,1]{2,1,0:T(1,128)} %broadcast_in_dim.23), calls=%async_computation | async-start | bytes 16384 | tf_op jit(solution)/shard_map/all_to_all | solution.py:15
  9.5 7.4 %while.16 = (s32[]{:T(128)}, f32[512,256]{1,0:T(8,128)S(1)}, s32[512]{0:T(512)S(1)}, s32[2048]{0:T(1024)}, f32[2048,256]{1,0:T(8,128)}, /*index=5*/s32[]{:T(128)}, s32[]{:T(128)}, s32[]{:T(128)}, s32[]{:T(128)}) while((s32[]{:T(128)}, f32[512,256]{1,0:T(8,128)S(1)}, s32[512]{0:T(512)S(1)}, s32[2048]{0:T(1024)}, ...), condition=%wide.region_4.5_spmd.clone, body=%wide.region_2.4_spmd.clone.sunk | while | flops 1612972544 | bytes 2121894 | solution.py:80
  9.5 0.7 dynamic_slice.64
  10.5 2.7 %fusion.28 = f32[512,256]{1,0:T(8,128)S(1)} fusion(f32[2048,256]{1,0:T(8,128)} %get-tuple-element.203, s32[]{:T(128)S(6)} %select_n.103, s32[1024]{0:T(1024)S(1)} %dynamic_slice.64, f32[512,256]{1,0:T(8,128)S(1)} %get-tuple-element.191, pred[]{:T(512)S(6)} %compare.20), kind=kOutput, calls=%fused_computation.8.clone.1 | convolution fusion | flops 1611399168 | bytes 2101253 | tf_op jit(solution)/shard_map/while/body/eval_jaxpr/dot_general | solution.py:71
  13.2 0.7 dynamic_slice.64
  14.2 2.7 %fusion.28 = f32[512,256]{1,0:T(8,128)S(1)} fusion(f32[2048,256]{1,0:T(8,128)} %get-tuple-element.203, s32[]{:T(128)S(6)} %select_n.103, s32[1024]{0:T(1024)S(1)} %dynamic_slice.64, f32[512,256]{1,0:T(8,128)S(1)} %get-tuple-element.191, pred[]{:T(512)S(6)} %compare.20), kind=kOutput, calls=%fused_computation.8.clone.1 | convolution fusion | flops 1611399168 | bytes 2101253 | tf_op jit(solution)/shard_map/while/body/eval_jaxpr/dot_general | solution.py:71
  16.9 0.5 broadcast.229
  17.4 0.7 reduce.8
  18.1 0.4 reduce.2
  18.5 0.6 broadcast_in_dim.24
  19.1 9.4 %all-to-all-start.1 = ((s32[16,16,1]{1,2,0:T(1,128)}), s32[16,16,1]{1,2,0:T(1,128)S(1)}, u32[]{:S(2)}, u32[]{:S(2)}) async-start(s32[16,16,1]{1,2,0:T(1,128)} %broadcast_in_dim.24), calls=%async_computation.1 | async-start | bytes 16384 | tf_op jit(solution)/shard_map/all_to_all | solution.py:15
  28.9 6.5 %all-to-all-done.1 = s32[16,16,1]{1,2,0:T(1,128)S(1)} async-done(((s32[16,16,1]{1,2,0:T(1,128)}), s32[16,16,1]{1,2,0:T(1,128)S(1)}, u32[]{:S(2)}, u32[]{:S(2)}) %all-to-all-start.1) | async-done | bytes 1056 | tf_op jit(solution)/shard_map/all_to_all | solution.py:15
  35.7 0.3 reduce-window.9
  36.3 0.6 dynamic_slice.21
  38.9 0.7 fusion.12
  39.8 1.5 %copy.44 = f32[256,2,1,1,258]{4,1,3,2,0:T(2,128)} copy(f32[256,2,1,1,258]{4,0,1,3,2:T(8,128)S(1)} %bitcast.46) | data formatting | bytes 1056768 | tf_op jit(solution)/shard_map/reshape | solution.py:42
  41.3 8.5 %all-to-all-start.2 = ((f32[256,2,1,1,258]{4,1,3,2,0:T(2,128)}), f32[256,2,1,1,258]{4,1,3,2,0:T(2,128)S(1)}, u32[]{:S(2)}, u32[]{:S(2)}) async-start(f32[256,2,1,1,258]{4,1,3,2,0:T(2,128)} %copy.44), calls=%async_computation.2 | async-start | bytes 1572864 | tf_op jit(solution)/shard_map/all_to_all | solution.py:43
  50.5 0.7 reduce_sum.22
  51.2 23.9 %all-to-all-done.2 = f32[256,2,1,1,258]{4,1,3,2,0:T(2,128)S(1)} async-done(((f32[256,2,1,1,258]{4,1,3,2,0:T(2,128)}), f32[256,2,1,1,258]{4,1,3,2,0:T(2,128)S(1)}, u32[]{:S(2)}, u32[]{:S(2)}) %all-to-all-start.2) | async-done | bytes 528416 | tf_op jit(solution)/shard_map/all_to_all | solution.py:43
  75.2 0.5 copy.47
  76.1 3.0 %scatter_custom_fusion.1 = s32[512]{0:T(512)} fusion(s32[512]{0:T(512)S(1)} %bitcast.49, s32[512]{0:T(512)S(1)} %bitcast.53, s32[]{:T(128)} %constant.105.clone.1), kind=kCustom, calls=%fused_computation.48 | custom fusion | bytes 2052 | tf_op jit(solution)/shard_map/scatter | solution.py:114
  79.1 3.0 %scatter_custom_fusion = f32[512,256]{1,0:T(8,128)} fusion(s32[512]{0:T(512)S(1)} %bitcast.50, f32[512,256]{1,0:T(8,128)S(1)} %bitcast.47, f32[]{:T(128)} %constant.95.clone.1), kind=kCustom, calls=%fused_computation.25 | custom fusion | bytes 524292 | tf_op jit(solution)/shard_map/scatter | solution.py:109
  82.1 3.0 %scatter_custom_fusion.2 = s32[512]{0:T(512)} fusion(s32[512]{0:T(512)S(1)} %bitcast.51, s32[512]{0:T(512)S(1)} %bitcast.52, s32[]{:T(128)} %constant.108.clone.1), kind=kCustom, calls=%fused_computation.46 | custom fusion | bytes 2052 | tf_op jit(solution)/shard_map/scatter | solution.py:119
  (40 shorter events, 3.0 us)
Async XLA Ops:
  1.9 16.2 %all-to-all-start = ((s32[16,1,1]{2,1,0:T(1,128)}), s32[16,1,1]{2,1,0:T(1,128)S(1)}, u32[]{:S(2)}, u32[]{:S(2)}) async-start(s32[16,1,1]{2,1,0:T(1,128)} %broadcast_in_dim.23), calls=%async_computation | async-start | bytes 16384 | tf_op jit(solution)/shard_map/all_to_all | solution.py:15
  9.5 7.9 %copy-start = (s32[1,512]{1,0:T(1,128)S(1)}, s32[1,512]{1,0:T(1,128)}, u32[]{:S(2)}) copy-start(s32[1,512]{1,0:T(1,128)} %param.8) | copy-start | bytes 6148
  19.1 16.4 %all-to-all-start.1 = ((s32[16,16,1]{1,2,0:T(1,128)}), s32[16,16,1]{1,2,0:T(1,128)S(1)}, u32[]{:S(2)}, u32[]{:S(2)}) async-start(s32[16,16,1]{1,2,0:T(1,128)} %broadcast_in_dim.24), calls=%async_computation.1 | async-start | bytes 16384 | tf_op jit(solution)/shard_map/all_to_all | solution.py:15
  41.3 33.8 %all-to-all-start.2 = ((f32[256,2,1,1,258]{4,1,3,2,0:T(2,128)}), f32[256,2,1,1,258]{4,1,3,2,0:T(2,128)S(1)}, u32[]{:S(2)}, u32[]{:S(2)}) async-start(f32[256,2,1,1,258]{4,1,3,2,0:T(2,128)} %copy.44), calls=%async_computation.2 | async-start | bytes 1572864 | tf_op jit(solution)/shard_map/all_to_all | solution.py:43
where the time goes:
time: 85.5 us; the launch traced here: 85.1 us
  waiting for transfers between devices  30.4 us (36%)
  starting transfers between devices  25.5 us (30%)
  local copies, waits for them, and re-layouts  16.7 us (20%)
  matrix products  5.36 us (6%)
  other arithmetic  3.76 us (4%)
  between operations  3.41 us (4%)
    all_to_all x1, waiting for transfers between devices, one_exchange(): tiles = lax.all_to_all(tiles, axis, split_axis=0, concat_axis=0, tiled=True)  23.9 us
    all_to_all x2, starting transfers between devices, copy_for_each(): return lax.all_to_all(copies, axis, split_axis=0, concat_axis=0, tiled=True)  17 us
    all_to_all x1, starting transfers between devices, one_exchange(): tiles = lax.all_to_all(tiles, axis, split_axis=0, concat_axis=0, tiled=True)  8.46 us
    all_to_all x2, waiting for transfers between devices, copy_for_each(): return lax.all_to_all(copies, axis, split_axis=0, concat_axis=0, tiled=True)  6.53 us
    dot_general x2, matrix products, accumulate(): jnp.dot(hits.astype(jnp.float32), values, precision=lax.Precision.HIGHEST...  5.36 us
    scatter x1, local copies, waits for them, and re-layouts, shards(): group_sums = jnp.zeros((span, width), jnp.float32).at[target].set(got_sum...  3.02 us
    scatter x1, local copies, waits for them, and re-layouts, shards(): group_rows = jnp.zeros((span,), jnp.int32).at[target].set(got_fields[:, 0...  3 us
    scatter x1, local copies, waits for them, and re-layouts, shards(): group_keys = jnp.full((span,), -1, jnp.int32).at[target].set(got_fields[:...  2.99 us
  transfers between devices with their start and end apart: 3, of which 2 were waited for; matrix products, arithmetic and copies ran while one was open for 12% of the time, Pallas kernels for 0%

commit v1 on v0

v1 whole, which is shorter than its diff:
```python
import functools

import jax
import jax.numpy as jnp
from jax import lax
from jax.experimental import pallas as pl
from jax.experimental.pallas import tpu as pltpu
from jax.sharding import PartitionSpec as P

AXES = ("gx", "gy", "gz")
MESH = pl.DeviceIdType.MESH
F32, BF16, I32 = jnp.float32, jnp.bfloat16, jnp.int32
CHUNKS = 4


def split2(v):
    hi = v.astype(BF16)
    lo = (v - hi.astype(F32)).astype(BF16)
    return hi, lo


def split3(v):
    hi = v.astype(BF16)
    rest = v - hi.astype(F32)
    mid = rest.astype(BF16)
    lo = (rest - mid.astype(F32)).astype(BF16)
    return hi, mid, lo


def dot(a, b):
    return jnp.dot(a, b, preferred_element_type=F32)


def kernel(
    sizes,
    measures, index, keys, count,
    out_sums, out_rows, out_keys, out_total,
    values, acc, tally, doubled, fields, outgoing, arrived, fsend, frecv, frelay, farrived,
    crow, cline, crelay, call,
    load_sems, cz_send, cz_recv, cp_send, cp_recv, fp_send, fp_recv, fz_send, fz_recv, b_send, b_recv,
):
    nx, ny, nz = sizes
    plane, devices = nx * ny, nx * ny * nz
    rows = measures.shape[0]
    step = rows // CHUNKS
    span = 2 * devices
    x, y, z = (lax.axis_index(a) for a in AXES)
    q = x * ny + y
    me = q * nz + z

    def in_line(k):
        return (z + k) % nz

    def in_plane(k):
        return (x + k // ny) % nx, (y + k % ny) % ny

    loads = [
        pltpu.make_async_copy(
            measures.at[pl.ds(c * step, step)], values.at[pl.ds(c * step, step)], load_sems.at[c]
        )
        for c in range(CHUNKS)
    ]
    for load in loads:
        load.start()

    barrier = pltpu.get_barrier_semaphore()
    for k in range(1, nz):
        pl.semaphore_signal(barrier, inc=1, device_id=(x, y, in_line(k)), device_id_type=MESH)

    @pl.loop(1, plane)
    def _(k):
        px, py = in_plane(k)
        pl.semaphore_signal(barrier, inc=1, device_id=(px, py, z), device_id_type=MESH)

    lane = lax.broadcasted_iota(I32, (1, 128), 1)
    mine = jnp.where(lane == me % 128, count[0], 0)
    crow[0] = mine
    cline[z] = mine

    labels = lax.broadcasted_iota(I32, (span, step), 0)
    ones = jnp.ones((step, 128), BF16)

    def accumulate(c):
        loads[c].wait()
        hits = jnp.where(labels == index[0:1, c * step : (c + 1) * step], 1.0, 0.0).astype(BF16)
        hi, lo = split2(values[pl.ds(c * step, step)])
        part = dot(hits, hi) + dot(hits, lo)
        seen = dot(hits, ones)
        if c == 0:
            acc[...] = part
            tally[...] = seen
        else:
            acc[...] += part
            tally[...] += seen

    accumulate(0)
    accumulate(1)
    pl.semaphore_wait(barrier, nz - 1 + plane - 1)

    for k in range(1, nz):
        pltpu.make_async_remote_copy(
            crow.at[0], cline.at[z], cz_send, cz_recv, device_id=(x, y, in_line(k)), device_id_type=MESH
        ).start()
    accumulate(2)
    accumulate(3)

    def drain(ref, n, sem):
        pltpu.make_async_copy(ref.at[pl.ds(0, n)], ref.at[pl.ds(0, n)], sem).wait()

    drain(cline, nz - 1, cz_recv)
    relayed = cline[0]
    for k in range(1, nz):
        relayed = relayed + cline[k]
    crelay[0] = relayed
    call[q] = relayed

    @pl.loop(1, plane)
    def _(k):
        px, py = in_plane(k)
        pltpu.make_async_remote_copy(
            crelay.at[0], call.at[q], cp_send, cp_recv, device_id=(px, py, z), device_id_type=MESH
        ).start()

    for level in range(2):
        for half in range(2):
            part = acc[pl.ds(level * devices, devices), pl.ds(half * 128, 128)]
            doubled[pl.ds(0, devices), 2 * level + half, :] = part
            doubled[pl.ds(devices, devices), 2 * level + half, :] = part
    flane = lax.broadcasted_iota(I32, (devices, 128), 1)
    tall_keys = jnp.broadcast_to(keys[...].astype(F32) + 1.0, (128, span)).T
    field = jnp.zeros((devices, 128), F32)
    for level in range(2):
        held = pl.ds(level * devices, devices)
        field = jnp.where(flane == level * 32 + q, tally[held, :], field)
        field = jnp.where(
            flane == 64 + level * 32 + q, tall_keys[level * devices : (level + 1) * devices], field
        )
    fields[pl.ds(0, devices), :] = field
    fields[pl.ds(devices, devices), :] = field

    drain(call, plane - 1, cp_recv)
    low = jnp.sum(call[pl.ds(0, plane // 2)], axis=0)
    high = jnp.sum(call[pl.ds(plane // 2, plane // 2)], axis=0)
    counts = jnp.concatenate([low, high], axis=1)
    lanes = lax.broadcasted_iota(I32, (1, devices), 1)
    offset = jnp.sum(jnp.where(lanes < me, counts, 0))
    start = devices - offset % devices
    fsend[...] = fields[pl.ds(start, devices), :].reshape(plane, nz, 128)

    @pl.loop(1, plane)
    def _(k):
        px, py = in_plane(k)
        pltpu.make_async_remote_copy(
            fsend.at[px * ny + py], frecv.at[q], fp_send, fp_recv, device_id=(px, py, z), device_id_type=MESH
        ).start()

    outgoing[...] = doubled[pl.ds(start, devices)]

    def send_block(k):
        i = k % nz
        dz = nz // 2 + jnp.where(i % 2 == 1, -((i + 1) // 2), i // 2)
        tz = (z + jnp.where(i == nz - 1, 0, dz)) % nz
        px, py = in_plane(plane - 1 - k // nz)
        target = (px * ny + py) * nz + tz
        pltpu.make_async_remote_copy(
            outgoing.at[target], arrived.at[me], b_send, b_recv, device_id=(px, py, tz), device_id_type=MESH
        ).start()

    pl.loop(0, devices // 2)(send_block)

    frecv[q] = fsend[q]
    drain(frecv, plane - 1, fp_recv)
    gathered = jnp.sum(frecv[...], axis=0)
    for k in range(nz):
        frelay[k] = gathered[k : k + 1]
    farrived[z] = frelay[z]
    for k in range(1, nz):
        pltpu.make_async_remote_copy(
            frelay.at[in_line(k)], farrived.at[z], fz_send, fz_recv, device_id=(x, y, in_line(k)), device_id_type=MESH
        ).start()

    pl.loop(devices // 2, devices - 1)(send_block)
    arrived[me] = outgoing[me]

    before = lax.broadcasted_iota(I32, (devices, devices), 0) < lax.broadcasted_iota(I32, (devices, devices), 1)
    before = jnp.where(before, 1.0, 0.0).astype(BF16)
    tops = jnp.broadcast_to((counts // 8).astype(F32).astype(BF16), (8, devices))
    rests = jnp.broadcast_to((counts % 8).astype(F32).astype(BF16), (8, devices))
    offsets = (8.0 * dot(tops, before) + dot(rests, before))[0:1].astype(I32)
    out_total[...] = jnp.sum(counts).reshape(1, 1)
    places = []
    for level in range(2):
        position = level * devices + (me - offsets) % devices
        place = (offsets + position) // devices
        places.append(jnp.where(position < counts, place, -1))
    place = jnp.concatenate(places, axis=1)
    picks = jnp.where(lax.broadcasted_iota(I32, (span, span), 0) == place, 1.0, 0.0).astype(BF16)

    drain(farrived, nz - 1, fz_recv)
    got = jnp.concatenate([farrived[k] for k in range(nz)], axis=0)
    wide = jnp.broadcast_to(got[None], (plane, nz, 128)).reshape(devices, 128)
    sender = lax.broadcasted_iota(I32, (devices, 128), 0) // nz
    fit = flane % 32 == sender
    in_level = (flane // 32) % 2
    chosen = jnp.concatenate(
        [jnp.where(fit & (in_level == level), wide, 0.0) for level in range(2)], axis=0
    )
    hi, mid, lo = split3(chosen)
    found = ((dot(picks, hi) + dot(picks, mid)) + dot(picks, lo)).T
    out_rows[...] = jnp.sum(found[0:64], axis=0, keepdims=True).astype(I32)
    out_keys[...] = jnp.sum(found[64:128], axis=0, keepdims=True).astype(I32) - 1

    drain(arrived, devices - 1, b_recv)
    parts = []
    for level in range(2):
        parts.append(
            jnp.concatenate([arrived[:, 2 * level + half, :] for half in range(2)], axis=1)
        )
    hi, lo = split2(jnp.concatenate(parts, axis=0))
    out_sums[...] = dot(picks, hi) + dot(picks, lo)

    drain(cline, nz - 1, cz_send)
    drain(call, plane - 1, cp_send)
    drain(fsend, plane - 1, fp_send)
    drain(farrived, nz - 1, fz_send)
    drain(outgoing, devices - 1, b_send)


def solution(mesh):
    sizes = tuple(mesh.shape[a] for a in AXES)
    nx, ny, nz = sizes
    plane, devices = nx * ny, nx * ny * nz
    vmem = pl.BlockSpec(memory_space=pltpu.VMEM)

    def shards(measures, group_index, distinct_keys, group_counts):
        rows, width = measures.shape
        span = distinct_keys.shape[1]
        sums, tallies, keys, total = pl.pallas_call(
            functools.partial(kernel, sizes),
            out_shape=(
                jax.ShapeDtypeStruct((span, width), F32),
                jax.ShapeDtypeStruct((1, span), I32),
                jax.ShapeDtypeStruct((1, span), I32),
                jax.ShapeDtypeStruct((1, 1), I32),
            ),
            in_specs=[
                pl.BlockSpec(memory_space=pl.ANY),
                vmem,
                vmem,
                pl.BlockSpec(memory_space=pltpu.SMEM),
            ],
            out_specs=(vmem, vmem, vmem, vmem),
            scratch_shapes=[
                pltpu.VMEM((rows, width), F32),
                pltpu.VMEM((span, width), F32),
                pltpu.VMEM((span, 128), F32),
                pltpu.VMEM((span, 4, 128), F32),
                pltpu.VMEM((span, 128), F32),
                pltpu.VMEM((devices, 4, 128), F32),
                pltpu.VMEM((devices, 4, 128), F32),
                pltpu.VMEM((plane, nz, 128), F32),
                pltpu.VMEM((plane, nz, 128), F32),
                pltpu.VMEM((nz, 1, 128), F32),
                pltpu.VMEM((nz, 1, 128), F32),
                pltpu.VMEM((1, 1, 128), I32),
                pltpu.VMEM((nz, 1, 128), I32),
                pltpu.VMEM((1, 1, 128), I32),
                pltpu.VMEM((plane, 1, 128), I32),
                pltpu.SemaphoreType.DMA((CHUNKS,)),
            ]
            + [pltpu.SemaphoreType.DMA(())] * 10,
            compiler_params=pltpu.CompilerParams(collective_id=0, has_side_effects=True),
            name="groups",
        )(measures, group_index.reshape(1, rows), distinct_keys, group_counts)
        return sums, tallies.reshape(span), keys.reshape(span), total.reshape(())

    return jax.shard_map(
        shards,
        mesh=mesh,
        in_specs=(P(AXES, None), P(AXES), P(AXES, None), P(AXES)),
        out_specs=(P(AXES, None), P(AXES), P(AXES), P()),
        check_vma=False,
    )
```

time: 85.5 us -> 46.5 us (0.54)
  Pallas kernels: 0 us -> 38.9 us
  waiting for transfers between devices: 30.4 us -> 0 us
  starting transfers between devices: 25.5 us -> 0 us
  local copies, waits for them, and re-layouts: 16.7 us -> 4.37 us
  matrix products: 5.36 us -> 0 us
  other arithmetic: 3.76 us -> 0 us
    pallas_call x0 -> x1, Pallas kernels: none -> 38.9 us  [shards(): pl.pallas_call(functools.partial(kernel, sizes), out_shape=(jax.ShapeDtyp...]
    all_to_all x3 -> x0, waiting for transfers between devices: 30.4 us -> none  [the longest x1 23.9 us: one_exchange(): tiles = lax.all_to_all(tiles, axis, split_axis=0, concat_axis=0, tiled=True)]
    all_to_all x3 -> x0, starting transfers between devices: 25.5 us -> none  [the longest x2 17 us: copy_for_each(): return lax.all_to_all(copies, axis, split_axis=0, concat_axis=0, tiled=True)]
    scatter x3 -> x0, local copies, waits for them, and re-layouts: 9.01 us -> none  [the longest x1 3.02 us: shards(): group_sums = jnp.zeros((span, width), jnp.float32).at[target].set(got_sum...]
    dot_general x2 -> x0, matrix products: 5.36 us -> none  [accumulate(): jnp.dot(hits.astype(jnp.float32), values, precision=lax.Precision.HIGHEST...]
    unnamed x3, local copies, waits for them, and re-layouts: 0.52 us -> 4.37 us
    dynamic_slice x3 -> x0, local copies, waits for them, and re-layouts: 1.98 us -> none  [the longest x2 1.38 us: accumulate(): index = lax.dynamic_slice_in_dim(group_index, start, block)]
    reshape x3 -> x0, local copies, waits for them, and re-layouts: 1.67 us -> none  [the longest x1 1.48 us: one_exchange(): tiles = tiles.reshape(-1, *inside)]
  transfers between devices with their start and end apart: 3 -> 0, of which waited for: 2 -> 0; matrix products, arithmetic and copies ran while one was open for 12% -> 0% of each run, Pallas kernels for 0% -> 0%
where the time goes in v1:
time: 46.5 us; the launch traced here: 46.2 us
  Pallas kernels  38.9 us (84%)
  local copies, waits for them, and re-layouts  4.37 us (9%)
  between operations  3.02 us (6%)
    pallas_call x1, Pallas kernels, shards(): pl.pallas_call(functools.partial(kernel, sizes), out_shape=(jax.ShapeDtyp...  38.9 us
    unnamed x3, local copies, waits for them, and re-layouts  4.37 us

profile of v1, /device:TPU:1, one launch (start us, length us, event | category | flops | bytes accessed | tf_op | source)
XLA Modules:
  0.0 46.2 jit_solution(8722270669430865083)
XLA Ops:
  1.3 38.9 %groups.1 = (f32[512,256]{1,0:T(8,128)}, s32[1,512]{1,0:T(1,128)}, s32[1,512]{1,0:T(1,128)}, s32[1,1]{1,0:T(1,128)}) custom-call(f32[2048,256]{1,0:T(8,128)} %measures.1, s32[1,2048]{1,0:T(1,128)} %bitcast.4, s32[1,512]{1,0:T(1,128)} %keys.1, s32[1]{0:T(128)S(6)} %copy.12.count), custom_call_target="tpu_custom_call" | custom-call | tf_op jit(solution)/shard_map/groups/pallas_call | solution.py:238
  40.1 1.9 %copy.13 = f32[512,256]{1,0:T(8,128)} copy(f32[512,256]{1,0:T(8,128)} %get-tuple-element.16) | data formatting | bytes 1048576
  42.0 1.3 %copy.14 = s32[512]{0:T(512)} copy(s32[512]{0:T(512)} %bitcast.6) | data formatting | bytes 4096
  43.3 1.2 %copy.15 = s32[512]{0:T(512)} copy(s32[512]{0:T(512)} %bitcast.5) | data formatting | bytes 4096

commit v2 on v1

v2 whole, which is shorter than its diff:
```python
import functools

import jax
import jax.numpy as jnp
from jax import lax
from jax.experimental import pallas as pl
from jax.experimental.pallas import tpu as pltpu
from jax.sharding import PartitionSpec as P

AXES = ("gx", "gy", "gz")
MESH = pl.DeviceIdType.MESH
F32, BF16, I32 = jnp.float32, jnp.bfloat16, jnp.int32
CHUNKS = 4
FIRST = 20


def split2(v):
    hi = v.astype(BF16)
    lo = (v - hi.astype(F32)).astype(BF16)
    return hi, lo


def split3(v):
    hi = v.astype(BF16)
    rest = v - hi.astype(F32)
    mid = rest.astype(BF16)
    lo = (rest - mid.astype(F32)).astype(BF16)
    return hi, mid, lo


def dot(a, b):
    return jnp.dot(a, b, preferred_element_type=F32)


def kernel(
    sizes,
    measures, index_in, keys_in,
    arrived, small,
    values, index, keys, acc, tally, doubled, fields, outgoing, fsend, frecv, frelay, farrived,
    crow, cline, crelay, call,
    load_sems, own_sem, cz_send, cz_recv, cp_send, cp_recv, fp_send, fp_recv, fz_send, fz_recv, b_send, b_recv,
):
    nx, ny, nz = sizes
    plane, devices = nx * ny, nx * ny * nz
    rows = measures.shape[0]
    step = rows // CHUNKS
    span = 2 * devices
    x, y, z = (lax.axis_index(a) for a in AXES)
    q = x * ny + y
    me = q * nz + z

    def outward(n):
        return sorted(range(n), key=lambda k: -min(k, n - k))

    def moved(base, k, n):
        return lax.rem(base + k, n) if k else base

    lines = [(k, moved(z, k, nz)) for k in outward(nz) if k]
    across = sorted(
        ((i, j) for i in range(nx) for j in range(ny) if i or j),
        key=lambda t: -(min(t[0], nx - t[0]) + min(t[1], ny - t[1]) / 2),
    )
    xs = [moved(x, k, nx) for k in range(nx)]
    ys = [moved(y, k, ny) for k in range(ny)]
    peers = [(xs[i], ys[j]) for i, j in across]

    loads = [
        pltpu.make_async_copy(
            measures.at[pl.ds(c * step, step)], values.at[pl.ds(c * step, step)], load_sems.at[c]
        )
        for c in range(CHUNKS)
    ]
    inputs = [
        pltpu.make_async_copy(src, dst, load_sems.at[CHUNKS + i])
        for i, (src, dst) in enumerate(((index_in, index), (keys_in, keys)))
    ]
    for load in inputs + loads:
        load.start()

    barrier = pltpu.get_barrier_semaphore()
    for _, tz in lines:
        pl.semaphore_signal(barrier, inc=1, device_id=(x, y, tz), device_id_type=MESH)
    for px, py in peers:
        pl.semaphore_signal(barrier, inc=1, device_id=(px, py, z), device_id_type=MESH)

    for load in inputs:
        load.wait()
    count = jnp.max(index[...], axis=1, keepdims=True) + 1
    lane = lax.broadcasted_iota(I32, (1, 128), 1)
    mine = jnp.where(lane == me % 128, count, 0)
    crow[0] = mine
    cline[z] = mine

    labels = lax.broadcasted_iota(I32, (span, step), 0)
    ones = jnp.ones((step, 128), BF16)

    def accumulate(c):
        loads[c].wait()
        hits = jnp.where(labels == index[0:1, c * step : (c + 1) * step], 1.0, 0.0).astype(BF16)
        hi, lo = split2(values[pl.ds(c * step, step)])
        part = dot(hits, hi) + dot(hits, lo)
        seen = dot(hits, ones)
        if c == 0:
            acc[...] = part
            tally[...] = seen
        else:
            acc[...] += part
            tally[...] += seen

    accumulate(0)
    accumulate(1)
    pl.semaphore_wait(barrier, nz - 1 + plane - 1)

    for _, tz in lines:
        pltpu.make_async_remote_copy(
            crow.at[0], cline.at[z], cz_send, cz_recv, device_id=(x, y, tz), device_id_type=MESH
        ).start()
    accumulate(2)
    accumulate(3)

    def drain(ref, n, sem):
        pltpu.make_async_copy(ref.at[pl.ds(0, n)], ref.at[pl.ds(0, n)], sem).wait()

    drain(cline, nz - 1, cz_recv)
    relayed = cline[0]
    for k in range(1, nz):
        relayed = relayed + cline[k]
    crelay[0] = relayed
    call[q] = relayed

    for px, py in peers:
        pltpu.make_async_remote_copy(
            crelay.at[0], call.at[q], cp_send, cp_recv, device_id=(px, py, z), device_id_type=MESH
        ).start()

    for level in range(2):
        for half in range(2):
            part = acc[pl.ds(level * devices, devices), pl.ds(half * 128, 128)]
            doubled[pl.ds(0, devices), 2 * level + half, :] = part
            doubled[pl.ds(devices, devices), 2 * level + half, :] = part
    flane = lax.broadcasted_iota(I32, (devices, 128), 1)
    tall_keys = jnp.broadcast_to(keys[...].astype(F32) + 1.0, (128, span)).T
    low_half, high_half = pl.ds(0, devices), pl.ds(devices, devices)
    kind = lax.rem(flane, 4)
    field = jnp.where(
        kind < 2,
        jnp.where(kind == 0, tally[low_half, :], tally[high_half, :]),
        jnp.where(kind == 2, tall_keys[:devices], tall_keys[devices:]),
    )
    fields[pl.ds(0, devices), :] = field
    fields[pl.ds(devices, devices), :] = field

    drain(call, plane - 1, cp_recv)
    low = jnp.sum(call[pl.ds(0, plane // 2)], axis=0)
    high = jnp.sum(call[pl.ds(plane // 2, plane // 2)], axis=0)
    counts = jnp.concatenate([low, high], axis=1)
    lanes = lax.broadcasted_iota(I32, (1, devices), 1)
    offset = jnp.sum(jnp.where(lanes < me, counts, 0))
    start = devices - offset % devices
    outgoing[...] = doubled[pl.ds(start, devices)]
    line_id = lax.rem(lax.broadcasted_iota(I32, (devices, 128), 0), nz)
    mark = lax.div(flane, 4) == lax.rem(line_id + q, plane)
    rolled = jnp.where(mark, fields[pl.ds(start, devices), :], 0.0).reshape(plane, nz, 128)
    fsend[...] = jnp.sum(rolled, axis=1, keepdims=True)

    def send_block(px, py, tz):
        target = (px * ny + py) * nz + tz
        pltpu.make_async_remote_copy(
            outgoing.at[target], arrived.at[me], b_send, b_recv, device_id=(px, py, tz), device_id_type=MESH
        ).start()

    def far_first(i, n):
        return n // 2 + jnp.where(lax.rem(i, 2) == 1, -lax.div(i + 1, 2), lax.div(i, 2))

    def send_blocks(i):
        px = lax.rem(x + far_first(lax.div(i, ny), nx), nx)
        py = lax.rem(y + far_first(lax.rem(i, ny), ny), ny)
        for _, tz in lines:
            send_block(px, py, tz)
        send_block(px, py, z)

    for px, py in peers:
        pltpu.make_async_remote_copy(
            fsend.at[px * ny + py], frecv.at[q], fp_send, fp_recv, device_id=(px, py, z), device_id_type=MESH
        ).start()
    pl.loop(0, FIRST)(send_blocks)
    frecv[q] = fsend[q]
    drain(frecv, plane - 1, fp_recv)
    got = frecv[...].reshape(plane, 128)
    group = lax.div(lax.broadcasted_iota(I32, (plane, 128), 1), 4)
    source = lax.broadcasted_iota(I32, (plane, 128), 0)
    for k in range(nz):
        frelay[k] = jnp.sum(jnp.where(group == lax.rem(source + k, plane), got, 0.0), axis=0, keepdims=True)
    farrived[z] = frelay[z]
    for _, tz in lines:
        pltpu.make_async_remote_copy(
            frelay.at[tz], farrived.at[z], fz_send, fz_recv, device_id=(x, y, tz), device_id_type=MESH
        ).start()
    pl.loop(FIRST, plane - 1)(send_blocks)
    for _, tz in lines:
        send_block(x, y, tz)
    own = pltpu.make_async_copy(outgoing.at[me], arrived.at[me], own_sem)
    own.start()

    before = lax.broadcasted_iota(I32, (devices, devices), 0) < lax.broadcasted_iota(I32, (devices, devices), 1)
    before = jnp.where(before, 1.0, 0.0).astype(BF16)
    tops = jnp.broadcast_to((counts // 8).astype(F32).astype(BF16), (8, devices))
    rests = jnp.broadcast_to((counts % 8).astype(F32).astype(BF16), (8, devices))
    offsets = (8.0 * dot(tops, before) + dot(rests, before))[0:1].astype(I32)
    places = []
    for level in range(2):
        position = level * devices + (me - offsets) % devices
        place = (offsets + position) // devices
        places.append(jnp.where(position < counts, place, -1))
    place = jnp.concatenate(places, axis=1)
    picks = jnp.where(lax.broadcasted_iota(I32, (span, span), 0) == place, 1.0, 0.0).astype(BF16)

    drain(farrived, nz - 1, fz_recv)
    got = jnp.concatenate([farrived[k] for k in range(nz)], axis=0)
    wide = jnp.broadcast_to(got[None], (plane, nz, 128)).reshape(devices, 128)
    sender = lax.div(lax.broadcasted_iota(I32, (devices, 128), 0), nz)
    fit = lax.div(flane, 4) == lax.rem(sender + z, plane)
    chosen = jnp.concatenate(
        [jnp.where(fit & (lax.rem(flane, 2) == level), wide, 0.0) for level in range(2)], axis=0
    )
    hi, mid, lo = split3(chosen)
    found = ((dot(picks, hi) + dot(picks, mid)) + dot(picks, lo)).T
    is_key = lax.rem(lax.broadcasted_iota(I32, (128, span), 0), 4) >= 2
    small[0:1] = jnp.sum(jnp.where(is_key, 0.0, found), axis=0, keepdims=True).astype(I32)
    small[1:2] = jnp.sum(jnp.where(is_key, found, 0.0), axis=0, keepdims=True).astype(I32) - 1
    small[2:3] = place
    small[3:4] = jnp.broadcast_to(jnp.sum(counts, axis=1, keepdims=True), (1, span))
    own.wait()
    drain(arrived, devices - 1, b_recv)
    drain(cline, nz - 1, cz_send)
    drain(call, plane - 1, cp_send)
    drain(fsend, plane - 1, fp_send)
    drain(farrived, nz - 1, fz_send)
    drain(outgoing, devices - 1, b_send)


def put(arrived, small, out_sums, out_rows, out_keys, out_total):
    span = out_sums.shape[0]
    out_rows[...] = small[0:1]
    out_keys[...] = small[1:2]
    out_total[...] = small[3:4, 0:1]
    picks = jnp.where(lax.broadcasted_iota(I32, (span, span), 0) == small[2:3], 1.0, 0.0).astype(BF16)
    parts = []
    for level in range(2):
        parts.append(
            jnp.concatenate([arrived[:, 2 * level + half, :] for half in range(2)], axis=1)
        )
    hi, lo = split2(jnp.concatenate(parts, axis=0))
    out_sums[...] = dot(picks, hi) + dot(picks, lo)


def solution(mesh):
    sizes = tuple(mesh.shape[a] for a in AXES)
    nx, ny, nz = sizes
    plane, devices = nx * ny, nx * ny * nz
    vmem = pl.BlockSpec(memory_space=pltpu.VMEM)

    def shards(measures, group_index, distinct_keys, group_counts):
        rows, width = measures.shape
        span = distinct_keys.shape[1]
        hbm = pl.BlockSpec(memory_space=pl.ANY)
        arrived, small = pl.pallas_call(
            functools.partial(kernel, sizes),
            out_shape=(
                jax.ShapeDtypeStruct((devices, 4, 128), F32),
                jax.ShapeDtypeStruct((8, span), I32),
            ),
            in_specs=[hbm] * 3,
            out_specs=(pl.BlockSpec(memory_space=pl.ANY), vmem),
            scratch_shapes=[
                pltpu.VMEM((rows, width), F32),
                pltpu.VMEM((1, rows), I32),
                pltpu.VMEM((1, span), I32),
                pltpu.VMEM((span, width), F32),
                pltpu.VMEM((span, 128), F32),
                pltpu.VMEM((span, 4, 128), F32),
                pltpu.VMEM((span, 128), F32),
                pltpu.VMEM((devices, 4, 128), F32),
                pltpu.VMEM((plane, 1, 128), F32),
                pltpu.VMEM((plane, 1, 128), F32),
                pltpu.VMEM((nz, 1, 128), F32),
                pltpu.VMEM((nz, 1, 128), F32),
                pltpu.VMEM((1, 1, 128), I32),
                pltpu.VMEM((nz, 1, 128), I32),
                pltpu.VMEM((1, 1, 128), I32),
                pltpu.VMEM((plane, 1, 128), I32),
                pltpu.SemaphoreType.DMA((CHUNKS + 2,)),
            ]
            + [pltpu.SemaphoreType.DMA(())] * 11,
            compiler_params=pltpu.CompilerParams(
                collective_id=0, has_side_effects=True, vmem_limit_bytes=32 << 20
            ),
            name="exchange",
        )(*(
            pltpu.with_memory_space_constraint(a, pltpu.MemorySpace.HBM)
            for a in (measures, group_index.reshape(1, rows), distinct_keys)
        ))
        sums, tallies, keys, total = pl.pallas_call(
            put,
            out_shape=(
                jax.ShapeDtypeStruct((span, width), F32),
                jax.ShapeDtypeStruct((1, span), I32),
                jax.ShapeDtypeStruct((1, span), I32),
                jax.ShapeDtypeStruct((1, 1), I32),
            ),
            in_specs=[vmem] * 2,
            out_specs=(vmem,) * 4,
            compiler_params=pltpu.CompilerParams(vmem_limit_bytes=24 << 20),
            name="put",
        )(arrived, small)
        return sums, tallies.reshape(span), keys.reshape(span), total.reshape(())

    return jax.shard_map(
        shards,
        mesh=mesh,
        in_specs=(P(AXES, None), P(AXES), P(AXES, None), P(AXES)),
        out_specs=(P(AXES, None), P(AXES), P(AXES), P()),
        check_vma=False,
    )
```

time: 46.5 us -> 37.1 us (0.80)
  local copies, waits for them, and re-layouts: 4.37 us -> 0 us
  Pallas kernels: 38.9 us -> 36.3 us
  between operations: 3.02 us -> 0.64 us
    unnamed x3 -> x0, local copies, waits for them, and re-layouts: 4.37 us -> none
    pallas_call x1, Pallas kernels: 38.9 us -> 34.9 us  [shards(): pl.pallas_call(functools.partial(kernel, sizes), out_shape=(jax.ShapeDtyp...]
    pallas_call x0 -> x1, Pallas kernels: none -> 1.39 us  [shards(): pl.pallas_call(put, out_shape=(jax.ShapeDtypeStruct((span, width), F32),...]
where the time goes in v2:
time: 37.1 us; the launch traced here: 37 us
  Pallas kernels  36.3 us (98%)
  between operations  0.64 us (2%)
    pallas_call x1, Pallas kernels, shards(): pl.pallas_call(functools.partial(kernel, sizes), out_shape=(jax.ShapeDtyp...  34.9 us
    pallas_call x1, Pallas kernels, shards(): pl.pallas_call(put, out_shape=(jax.ShapeDtypeStruct((span, width), F32),...  1.39 us

profile of v2, /device:TPU:1, one launch (start us, length us, event | category | flops | bytes accessed | tf_op | source)
XLA Modules:
  0.0 37.0 jit_solution(7055414296413262492)
XLA Ops:
  0.6 34.9 %exchange.1 = (f32[256,4,128]{2,1,0:T(4,128)S(1)}, s32[8,512]{1,0:T(8,128)S(1)}) custom-call(f32[2048,256]{1,0:T(8,128)} %measures.1, s32[1,2048]{1,0:T(1,128)} %bitcast.4, s32[1,512]{1,0:T(1,128)} %keys_in.1), custom_call_target="tpu_custom_call" | custom-call | tf_op jit(solution)/shard_map/exchange/pallas_call | solution.py:267
  35.6 1.4 %put.1 = (f32[512,256]{1,0:T(8,128)}, s32[1,512]{1,0:T(1,128)}, s32[1,512]{1,0:T(1,128)}, s32[1,1]{1,0:T(1,128)}) custom-call(f32[256,4,128]{2,1,0:T(4,128)S(1)} %get-tuple-element.10.arrived, s32[8,512]{1,0:T(8,128)S(1)} %get-tuple-element.11.small), custom_call_target="tpu_custom_call" | custom-call | tf_op jit(solution)/shard_map/put/pallas_call | solution.py:303

commit v3 on v2

--- a/solution.py
+++ b/solution.py
@@ -11,7 +11,7 @@
 MESH = pl.DeviceIdType.MESH
 F32, BF16, I32 = jnp.float32, jnp.bfloat16, jnp.int32
 CHUNKS = 4
-FIRST = 20
+EARLY, LATE = 24, 112
 
 
 def split2(v):
@@ -64,6 +64,12 @@
     ys = [moved(y, k, ny) for k in range(ny)]
     peers = [(xs[i], ys[j]) for i, j in across]
 
+    barrier = pltpu.get_barrier_semaphore()
+    for px, py in peers:
+        pl.semaphore_signal(barrier, inc=1, device_id=(px, py, z), device_id_type=MESH)
+    for _, tz in lines:
+        pl.semaphore_signal(barrier, inc=1, device_id=(x, y, tz), device_id_type=MESH)
+
     loads = [
         pltpu.make_async_copy(
             measures.at[pl.ds(c * step, step)], values.at[pl.ds(c * step, step)], load_sems.at[c]
@@ -77,12 +83,6 @@
     for load in inputs + loads:
         load.start()
 
-    barrier = pltpu.get_barrier_semaphore()
-    for _, tz in lines:
-        pl.semaphore_signal(barrier, inc=1, device_id=(x, y, tz), device_id_type=MESH)
-    for px, py in peers:
-        pl.semaphore_signal(barrier, inc=1, device_id=(px, py, z), device_id_type=MESH)
-
     for load in inputs:
         load.wait()
     count = jnp.max(index[...], axis=1, keepdims=True) + 1
@@ -107,16 +107,14 @@
             acc[...] += part
             tally[...] += seen
 
-    accumulate(0)
-    accumulate(1)
     pl.semaphore_wait(barrier, nz - 1 + plane - 1)
 
     for _, tz in lines:
         pltpu.make_async_remote_copy(
             crow.at[0], cline.at[z], cz_send, cz_recv, device_id=(x, y, tz), device_id_type=MESH
         ).start()
-    accumulate(2)
-    accumulate(3)
+    for c in range(CHUNKS):
+        accumulate(c)
 
     def drain(ref, n, sem):
         pltpu.make_async_copy(ref.at[pl.ds(0, n)], ref.at[pl.ds(0, n)], sem).wait()
@@ -158,32 +156,37 @@
     offset = jnp.sum(jnp.where(lanes < me, counts, 0))
     start = devices - offset % devices
     outgoing[...] = doubled[pl.ds(start, devices)]
+
+    def send_block(px, py, tz):
+        target = (px * ny + py) * nz + tz
+        pltpu.make_async_remote_copy(
+            outgoing.at[target], arrived.at[me], b_send, b_recv, device_id=(px, py, tz), device_id_type=MESH
+        ).start()
+
+    def hops(offset):
+        i, j, k = offset
+        return min(i, nx - i) + min(j, ny - j) / 2 + (j % 2) * 0.1 + min(k, nz - k)
+
+    order = sorted(
+        ((i, j, k) for i in range(nx) for j in range(ny) for k in range(nz) if i or j or k),
+        key=lambda t: (-hops(t), t),
+    )
+    zs = [moved(z, k, nz) for k in range(nz)]
+
+    def send_blocks(offsets):
+        for i, j, k in offsets:
+            send_block(xs[i], ys[j], zs[k])
+
+    send_blocks(order[:EARLY])
     line_id = lax.rem(lax.broadcasted_iota(I32, (devices, 128), 0), nz)
     mark = lax.div(flane, 4) == lax.rem(line_id + q, plane)
     rolled = jnp.where(mark, fields[pl.ds(start, devices), :], 0.0).reshape(plane, nz, 128)
     fsend[...] = jnp.sum(rolled, axis=1, keepdims=True)
-
-    def send_block(px, py, tz):
-        target = (px * ny + py) * nz + tz
-        pltpu.make_async_remote_copy(
-            outgoing.at[target], arrived.at[me], b_send, b_recv, device_id=(px, py, tz), device_id_type=MESH
-        ).start()
-
-    def far_first(i, n):
-        return n // 2 + jnp.where(lax.rem(i, 2) == 1, -lax.div(i + 1, 2), lax.div(i, 2))
-
-    def send_blocks(i):
-        px = lax.rem(x + far_first(lax.div(i, ny), nx), nx)
-        py = lax.rem(y + far_first(lax.rem(i, ny), ny), ny)
-        for _, tz in lines:
-            send_block(px, py, tz)
-        send_block(px, py, z)
-
     for px, py in peers:
         pltpu.make_async_remote_copy(
             fsend.at[px * ny + py], frecv.at[q], fp_send, fp_recv, device_id=(px, py, z), device_id_type=MESH
         ).start()
-    pl.loop(0, FIRST)(send_blocks)
+    send_blocks(order[EARLY:LATE])
     frecv[q] = fsend[q]
     drain(frecv, plane - 1, fp_recv)
     got = frecv[...].reshape(plane, 128)
@@ -196,9 +199,7 @@
         pltpu.make_async_remote_copy(
             frelay.at[tz], farrived.at[z], fz_send, fz_recv, device_id=(x, y, tz), device_id_type=MESH
         ).start()
-    pl.loop(FIRST, plane - 1)(send_blocks)
-    for _, tz in lines:
-        send_block(x, y, tz)
+    send_blocks(order[LATE:])
     own = pltpu.make_async_copy(outgoing.at[me], arrived.at[me], own_sem)
     own.start()
 
@@ -241,17 +242,22 @@
 
 def put(arrived, small, out_sums, out_rows, out_keys, out_total):
     span = out_sums.shape[0]
+    senders = span // 2
     out_rows[...] = small[0:1]
     out_keys[...] = small[1:2]
     out_total[...] = small[3:4, 0:1]
-    picks = jnp.where(lax.broadcasted_iota(I32, (span, span), 0) == small[2:3], 1.0, 0.0).astype(BF16)
-    parts = []
+    total = None
     for level in range(2):
-        parts.append(
-            jnp.concatenate([arrived[:, 2 * level + half, :] for half in range(2)], axis=1)
+        block = jnp.concatenate(
+            [arrived[pl.ds(2 * level + half, senders, stride=4), :] for half in range(2)], axis=1
         )
-    hi, lo = split2(jnp.concatenate(parts, axis=0))
-    out_sums[...] = dot(picks, hi) + dot(picks, lo)
+        hi, lo = split2(block)
+        places = small[2:3, level * senders : (level + 1) * senders]
+        labels = lax.broadcasted_iota(I32, (span, senders), 0)
+        picks = jnp.where(labels == places, 1.0, 0.0).astype(BF16)
+        part = dot(picks, hi) + dot(picks, lo)
+        total = part if total is None else total + part
+    out_sums[...] = total
 
 
 def solution(mesh):
@@ -312,7 +318,7 @@
             out_specs=(vmem,) * 4,
             compiler_params=pltpu.CompilerParams(vmem_limit_bytes=24 << 20),
             name="put",
-        )(arrived, small)
+        )(arrived.reshape(4 * devices, 128), small)
         return sums, tallies.reshape(span), keys.reshape(span), total.reshape(())
 
     return jax.shard_map(

time: 37.1 us -> 37 us (level)
  no operation moved by 1% of the time
where the time goes in v3:
time: 37 us; the launch traced here: 36.9 us
  Pallas kernels  36.3 us (98%)
  between operations  0.64 us (2%)
    pallas_call x1, Pallas kernels, shards(): pl.pallas_call(functools.partial(kernel, sizes), out_shape=(jax.ShapeDtyp...  35 us
    pallas_call x1, Pallas kernels, shards(): pl.pallas_call(put, out_shape=(jax.ShapeDtypeStruct((span, width), F32),...  1.26 us

profile of v3, /device:TPU:1, one launch (start us, length us, event | category | flops | bytes accessed | tf_op | source)
XLA Modules:
  0.0 36.9 jit_solution(16252039424540900945)
XLA Ops:
  0.6 35.0 %exchange.1 = (f32[256,4,128]{2,1,0:T(4,128)S(1)}, s32[8,512]{1,0:T(8,128)S(1)}) custom-call(f32[2048,256]{1,0:T(8,128)} %measures.1, s32[1,2048]{1,0:T(1,128)} %bitcast.6, s32[1,512]{1,0:T(1,128)} %keys_in.1), custom_call_target="tpu_custom_call" | custom-call | tf_op jit(solution)/shard_map/exchange/pallas_call | solution.py:273
  35.7 1.3 %put.1 = (f32[512,256]{1,0:T(8,128)}, s32[1,512]{1,0:T(1,128)}, s32[1,512]{1,0:T(1,128)}, s32[1,1]{1,0:T(1,128)}) custom-call(f32[1024,128]{1,0:T(8,128)S(1)} %bitcast.5, s32[8,512]{1,0:T(8,128)S(1)} %get-tuple-element.11.small), custom_call_target="tpu_custom_call" | custom-call | tf_op jit(solution)/shard_map/put/pallas_call | solution.py:309

commit v4 on v3

--- a/solution.py
+++ b/solution.py
@@ -36,9 +36,9 @@
     sizes,
     measures, index_in, keys_in,
     arrived, small,
-    values, index, keys, acc, tally, doubled, fields, outgoing, fsend, frecv, frelay, farrived,
+    values, index, keys, acc, tally, halves, near, fields, outgoing, fsend, frecv, frelay, farrived,
     crow, cline, crelay, call,
-    load_sems, own_sem, cz_send, cz_recv, cp_send, cp_recv, fp_send, fp_recv, fz_send, fz_recv, b_send, b_recv,
+    load_sems, own_sems, near_send, near_recv, cz_send, cz_recv, cp_send, cp_recv, fp_send, fp_recv, fz_send, fz_recv, b_send, b_recv,
 ):
     nx, ny, nz = sizes
     plane, devices = nx * ny, nx * ny * nz
@@ -119,6 +119,17 @@
     def drain(ref, n, sem):
         pltpu.make_async_copy(ref.at[pl.ds(0, n)], ref.at[pl.ds(0, n)], sem).wait()
 
+    for half in range(2):
+        for level in range(2):
+            part = acc[pl.ds(level * devices, devices), pl.ds(half * 128, 128)]
+            halves[half, level, pl.ds(0, devices), :] = part
+            halves[half, level, pl.ds(devices, devices), :] = part
+    for half, tz in ((0, moved(z, 1, nz)), (1, moved(z, nz - 1, nz))):
+        for level in range(2):
+            pltpu.make_async_remote_copy(
+                halves.at[half, level, pl.ds(0, devices)], near.at[half, level, pl.ds(0, devices)],
+                near_send, near_recv, device_id=(x, y, tz), device_id_type=MESH,
+            ).start()
     drain(cline, nz - 1, cz_recv)
     relayed = cline[0]
     for k in range(1, nz):
@@ -131,11 +142,6 @@
             crelay.at[0], call.at[q], cp_send, cp_recv, device_id=(px, py, z), device_id_type=MESH
         ).start()
 
-    for level in range(2):
-        for half in range(2):
-            part = acc[pl.ds(level * devices, devices), pl.ds(half * 128, 128)]
-            doubled[pl.ds(0, devices), 2 * level + half, :] = part
-            doubled[pl.ds(devices, devices), 2 * level + half, :] = part
     flane = lax.broadcasted_iota(I32, (devices, 128), 1)
     tall_keys = jnp.broadcast_to(keys[...].astype(F32) + 1.0, (128, span)).T
     low_half, high_half = pl.ds(0, devices), pl.ds(devices, devices)
@@ -153,29 +159,45 @@
     high = jnp.sum(call[pl.ds(plane // 2, plane // 2)], axis=0)
     counts = jnp.concatenate([low, high], axis=1)
     lanes = lax.broadcasted_iota(I32, (1, devices), 1)
-    offset = jnp.sum(jnp.where(lanes < me, counts, 0))
-    start = devices - offset % devices
-    outgoing[...] = doubled[pl.ds(start, devices)]
-
-    def send_block(px, py, tz):
-        target = (px * ny + py) * nz + tz
-        pltpu.make_async_remote_copy(
-            outgoing.at[target], arrived.at[me], b_send, b_recv, device_id=(px, py, tz), device_id_type=MESH
-        ).start()
+
+    def start_of(device):
+        return devices - lax.rem(jnp.sum(jnp.where(lanes < device, counts, 0)), devices)
+
+    start = start_of(me)
+    for level in range(2):
+        outgoing[0, pl.ds(level, devices, stride=4), :] = halves[1, level, pl.ds(start, devices), :]
+        outgoing[1, pl.ds(level, devices, stride=4), :] = halves[0, level, pl.ds(start, devices), :]
+    pltpu.make_async_copy(acc, acc, near_recv).wait()
+    for half, other in ((0, moved(z, nz - 1, nz)), (1, moved(z, 1, nz))):
+        first = start_of(q * nz + other)
+        for level in range(2):
+            near[half, level, pl.ds(devices, devices), :] = near[half, level, pl.ds(0, devices), :]
+            outgoing[half, pl.ds(2 + level, devices, stride=4), :] = near[half, level, pl.ds(first, devices), :]
+
+    reach = nz // 2
 
     def hops(offset):
-        i, j, k = offset
-        return min(i, nx - i) + min(j, ny - j) / 2 + (j % 2) * 0.1 + min(k, nz - k)
+        i, j, side, k = offset
+        return min(i, nx - i) + min(j, ny - j) / 2 + (j % 2) * 0.1 + k
 
     order = sorted(
-        ((i, j, k) for i in range(nx) for j in range(ny) for k in range(nz) if i or j or k),
+        (
+            (i, j, side, k)
+            for i in range(nx) for j in range(ny) for side in range(2) for k in range(reach) if i or j or k
+        ),
         key=lambda t: (-hops(t), t),
     )
     zs = [moved(z, k, nz) for k in range(nz)]
 
     def send_blocks(offsets):
-        for i, j, k in offsets:
-            send_block(xs[i], ys[j], zs[k])
+        for i, j, side, k in offsets:
+            px, py, tz = xs[i], ys[j], zs[(nz - k) % nz if side else k]
+            target = (px * ny + py) * nz + tz
+            pltpu.make_async_remote_copy(
+                outgoing.at[side, pl.ds(4 * target, 4)],
+                arrived.at[(side * plane + q) * reach + k],
+                b_send, b_recv, device_id=(px, py, tz), device_id_type=MESH,
+            ).start()
 
     send_blocks(order[:EARLY])
     line_id = lax.rem(lax.broadcasted_iota(I32, (devices, 128), 0), nz)
@@ -200,8 +222,14 @@
             frelay.at[tz], farrived.at[z], fz_send, fz_recv, device_id=(x, y, tz), device_id_type=MESH
         ).start()
     send_blocks(order[LATE:])
-    own = pltpu.make_async_copy(outgoing.at[me], arrived.at[me], own_sem)
-    own.start()
+    owns = [
+        pltpu.make_async_copy(
+            outgoing.at[side, pl.ds(4 * me, 4)], arrived.at[(side * plane + q) * reach], own_sems.at[side]
+        )
+        for side in range(2)
+    ]
+    for own in owns:
+        own.start()
 
     before = lax.broadcasted_iota(I32, (devices, devices), 0) < lax.broadcasted_iota(I32, (devices, devices), 1)
     before = jnp.where(before, 1.0, 0.0).astype(BF16)
@@ -229,35 +257,56 @@
     is_key = lax.rem(lax.broadcasted_iota(I32, (128, span), 0), 4) >= 2
     small[0:1] = jnp.sum(jnp.where(is_key, 0.0, found), axis=0, keepdims=True).astype(I32)
     small[1:2] = jnp.sum(jnp.where(is_key, found, 0.0), axis=0, keepdims=True).astype(I32) - 1
-    small[2:3] = place
-    small[3:4] = jnp.broadcast_to(jnp.sum(counts, axis=1, keepdims=True), (1, span))
-    own.wait()
-    drain(arrived, devices - 1, b_recv)
+    level_row = lax.broadcasted_iota(I32, (8, devices), 0)
+    natural = jnp.where(level_row == 0, place[:, :devices], place[:, devices:]).astype(F32) + 1.0
+    hi, lo = split2(natural)
+    slot = lax.broadcasted_iota(I32, (devices, devices), 1)
+    holder = lax.div(lax.rem(slot, devices // 2), reach)
+    shift = lax.rem(slot, reach)
+    direct = slot < devices // 2
+    for row, step_z in (
+        (2, jnp.where(direct, nz + shift, nz - shift - 1)),
+        (3, jnp.where(direct, nz - shift, nz + shift + 1)),
+    ):
+        source = holder * nz + lax.rem(z + step_z, nz)
+        match = lax.broadcasted_iota(I32, (devices, devices), 0) == source
+        match = jnp.where(match, 1.0, 0.0).astype(BF16)
+        ordered = (dot(hi, match) + dot(lo, match)).astype(I32) - 1
+        small[row : row + 1] = jnp.concatenate([ordered[0:1], ordered[1:2]], axis=1)
+    small[4:5] = jnp.broadcast_to(jnp.sum(counts, axis=1, keepdims=True), (1, span))
+    for own in owns:
+        own.wait()
+    drain(arrived, devices - 2, b_recv)
     drain(cline, nz - 1, cz_send)
     drain(call, plane - 1, cp_send)
     drain(fsend, plane - 1, fp_send)
     drain(farrived, nz - 1, fz_send)
-    drain(outgoing, devices - 1, b_send)
+    drain(arrived, devices - 2, b_send)
+    pltpu.make_async_copy(acc, acc, near_send).wait()
 
 
 def put(arrived, small, out_sums, out_rows, out_keys, out_total):
     span = out_sums.shape[0]
     senders = span // 2
+    slots = senders // 2
     out_rows[...] = small[0:1]
     out_keys[...] = small[1:2]
-    out_total[...] = small[3:4, 0:1]
-    total = None
-    for level in range(2):
-        block = jnp.concatenate(
-            [arrived[pl.ds(2 * level + half, senders, stride=4), :] for half in range(2)], axis=1
-        )
-        hi, lo = split2(block)
-        places = small[2:3, level * senders : (level + 1) * senders]
-        labels = lax.broadcasted_iota(I32, (span, senders), 0)
-        picks = jnp.where(labels == places, 1.0, 0.0).astype(BF16)
-        part = dot(picks, hi) + dot(picks, lo)
-        total = part if total is None else total + part
-    out_sums[...] = total
+    out_total[...] = small[4:5, 0:1]
+    labels = lax.broadcasted_iota(I32, (span, senders), 0)
+    sides = []
+    for half in range(2):
+        direct, relayed = (4 * slots, 2) if half == 0 else (0, 4 * slots + 2)
+        total = None
+        for level in range(2):
+            block = jnp.concatenate(
+                [arrived[pl.ds(base + level, slots, stride=4), :] for base in (direct, relayed)], axis=0
+            )
+            places = small[2 + half : 3 + half, level * senders : (level + 1) * senders]
+            picks = jnp.where(labels == places, 1.0, 0.0).astype(BF16)
+            part = dot(picks, jnp.concatenate(split2(block), axis=1))
+            total = part if total is None else total + part
+        sides.append(total[:, :128] + total[:, 128:])
+    out_sums[...] = jnp.concatenate(sides, axis=1)
 
 
 def solution(mesh):
@@ -284,9 +333,10 @@
                 pltpu.VMEM((1, span), I32),
                 pltpu.VMEM((span, width), F32),
                 pltpu.VMEM((span, 128), F32),
-                pltpu.VMEM((span, 4, 128), F32),
+                pltpu.VMEM((2, 2, span, 128), F32),
+                pltpu.VMEM((2, 2, span, 128), F32),
                 pltpu.VMEM((span, 128), F32),
-                pltpu.VMEM((devices, 4, 128), F32),
+                pltpu.VMEM((2, 4 * devices, 128), F32),
                 pltpu.VMEM((plane, 1, 128), F32),
                 pltpu.VMEM((plane, 1, 128), F32),
                 pltpu.VMEM((nz, 1, 128), F32),
@@ -296,8 +346,9 @@
                 pltpu.VMEM((1, 1, 128), I32),
                 pltpu.VMEM((plane, 1, 128), I32),
                 pltpu.SemaphoreType.DMA((CHUNKS + 2,)),
+                pltpu.SemaphoreType.DMA((2,)),
             ]
-            + [pltpu.SemaphoreType.DMA(())] * 11,
+            + [pltpu.SemaphoreType.DMA(())] * 12,
             compiler_params=pltpu.CompilerParams(
                 collective_id=0, has_side_effects=True, vmem_limit_bytes=32 << 20
             ),

time: 37 us -> 34.9 us (0.943)
  Pallas kernels: 36.3 us -> 34.2 us
    pallas_call x1, Pallas kernels: 35 us -> 32.9 us  [shards(): pl.pallas_call(functools.partial(kernel, sizes), out_shape=(jax.ShapeDtyp...]
where the time goes in v4:
time: 34.9 us; the launch traced here: 34.8 us
  Pallas kernels  34.2 us (98%)
  between operations  0.64 us (2%)
    pallas_call x1, Pallas kernels, shards(): pl.pallas_call(functools.partial(kernel, sizes), out_shape=(jax.ShapeDtyp...  32.9 us
    pallas_call x1, Pallas kernels, shards(): pl.pallas_call(put, out_shape=(jax.ShapeDtypeStruct((span, width), F32),...  1.24 us

profile of v4, /device:TPU:1, one launch (start us, length us, event | category | flops | bytes accessed | tf_op | source)
XLA Modules:
  0.0 34.8 jit_solution(10787855790642166791)
XLA Ops:
  0.6 32.9 %exchange.1 = (f32[256,4,128]{2,1,0:T(4,128)S(1)}, s32[8,512]{1,0:T(8,128)S(1)}) custom-call(f32[2048,256]{1,0:T(8,128)} %measures.1, s32[1,2048]{1,0:T(1,128)} %bitcast.6, s32[1,512]{1,0:T(1,128)} %keys_in.1), custom_call_target="tpu_custom_call" | custom-call | tf_op jit(solution)/shard_map/exchange/pallas_call | solution.py:322
  33.6 1.2 %put.1 = (f32[512,256]{1,0:T(8,128)}, s32[1,512]{1,0:T(1,128)}, s32[1,512]{1,0:T(1,128)}, s32[1,1]{1,0:T(1,128)}) custom-call(f32[1024,128]{1,0:T(8,128)S(1)} %bitcast.5, s32[8,512]{1,0:T(8,128)S(1)} %get-tuple-element.11.small), custom_call_target="tpu_custom_call" | custom-call | tf_op jit(solution)/shard_map/put/pallas_call | solution.py:360

commit v5 on v4

--- a/solution.py
+++ b/solution.py
@@ -11,7 +11,7 @@
 MESH = pl.DeviceIdType.MESH
 F32, BF16, I32 = jnp.float32, jnp.bfloat16, jnp.int32
 CHUNKS = 4
-EARLY, LATE = 24, 112
+LATE = 150
 
 
 def split2(v):
@@ -36,7 +36,7 @@
     sizes,
     measures, index_in, keys_in,
     arrived, small,
-    values, index, keys, acc, tally, halves, near, fields, outgoing, fsend, frecv, frelay, farrived,
+    values, index, keys, acc, tally, halves, near, outgoing, fsend, frecv, fown, fline,
     crow, cline, crelay, call,
     load_sems, own_sems, near_send, near_recv, cz_send, cz_recv, cp_send, cp_recv, fp_send, fp_recv, fz_send, fz_recv, b_send, b_recv,
 ):
@@ -92,6 +92,7 @@
     cline[z] = mine
 
     labels = lax.broadcasted_iota(I32, (span, step), 0)
+
     ones = jnp.ones((step, 128), BF16)
 
     def accumulate(c):
@@ -107,13 +108,15 @@
             acc[...] += part
             tally[...] += seen
 
+    for c in range(CHUNKS // 2):
+        accumulate(c)
     pl.semaphore_wait(barrier, nz - 1 + plane - 1)
 
     for _, tz in lines:
         pltpu.make_async_remote_copy(
             crow.at[0], cline.at[z], cz_send, cz_recv, device_id=(x, y, tz), device_id_type=MESH
         ).start()
-    for c in range(CHUNKS):
+    for c in range(CHUNKS // 2, CHUNKS):
         accumulate(c)
 
     def drain(ref, n, sem):
@@ -130,6 +133,16 @@
                 halves.at[half, level, pl.ds(0, devices)], near.at[half, level, pl.ds(0, devices)],
                 near_send, near_recv, device_id=(x, y, tz), device_id_type=MESH,
             ).start()
+    seen = tally[...].T[0:1]
+    named = keys[...].astype(F32) + 1.0
+    fown[0] = jnp.concatenate(
+        [row[:, level * devices : (level + 1) * devices] for row in (seen, named) for level in range(2)], axis=0
+    )
+    fline[z] = fown[0]
+    for _, tz in lines:
+        pltpu.make_async_remote_copy(
+            fown.at[0], fline.at[z], fz_send, fz_recv, device_id=(x, y, tz), device_id_type=MESH
+        ).start()
     drain(cline, nz - 1, cz_recv)
     relayed = cline[0]
     for k in range(1, nz):
@@ -142,18 +155,10 @@
             crelay.at[0], call.at[q], cp_send, cp_recv, device_id=(px, py, z), device_id_type=MESH
         ).start()
 
-    flane = lax.broadcasted_iota(I32, (devices, 128), 1)
-    tall_keys = jnp.broadcast_to(keys[...].astype(F32) + 1.0, (128, span)).T
-    low_half, high_half = pl.ds(0, devices), pl.ds(devices, devices)
-    kind = lax.rem(flane, 4)
-    field = jnp.where(
-        kind < 2,
-        jnp.where(kind == 0, tally[low_half, :], tally[high_half, :]),
-        jnp.where(kind == 2, tall_keys[:devices], tall_keys[devices:]),
-    )
-    fields[pl.ds(0, devices), :] = field
-    fields[pl.ds(devices, devices), :] = field
-
+    pltpu.make_async_copy(acc, acc, near_recv).wait()
+    for half in range(2):
+        for level in range(2):
+            near[half, level, pl.ds(devices, devices), :] = near[half, level, pl.ds(0, devices), :]
     drain(call, plane - 1, cp_recv)
     low = jnp.sum(call[pl.ds(0, plane // 2)], axis=0)
     high = jnp.sum(call[pl.ds(plane // 2, plane // 2)], axis=0)
@@ -167,11 +172,9 @@
     for level in range(2):
         outgoing[0, pl.ds(level, devices, stride=4), :] = halves[1, level, pl.ds(start, devices), :]
         outgoing[1, pl.ds(level, devices, stride=4), :] = halves[0, level, pl.ds(start, devices), :]
-    pltpu.make_async_copy(acc, acc, near_recv).wait()
     for half, other in ((0, moved(z, nz - 1, nz)), (1, moved(z, 1, nz))):
         first = start_of(q * nz + other)
         for level in range(2):
-            near[half, level, pl.ds(devices, devices), :] = near[half, level, pl.ds(0, devices), :]
             outgoing[half, pl.ds(2 + level, devices, stride=4), :] = near[half, level, pl.ds(first, devices), :]
 
     reach = nz // 2
@@ -199,27 +202,31 @@
                 b_send, b_recv, device_id=(px, py, tz), device_id_type=MESH,
             ).start()
 
-    send_blocks(order[:EARLY])
-    line_id = lax.rem(lax.broadcasted_iota(I32, (devices, 128), 0), nz)
-    mark = lax.div(flane, 4) == lax.rem(line_id + q, plane)
-    rolled = jnp.where(mark, fields[pl.ds(start, devices), :], 0.0).reshape(plane, nz, 128)
-    fsend[...] = jnp.sum(rolled, axis=1, keepdims=True)
+    send_blocks(order[:LATE])
+    drain(fline, nz - 1, fz_recv)
+    group = lax.broadcasted_iota(I32, (plane, devices), 1)
+    target = lax.broadcasted_iota(I32, (plane, devices), 0) * nz + z
+    picked = jnp.concatenate(
+        [
+            jnp.where(group == lax.rem(target + start_of(q * nz + k), devices), 1.0, 0.0).astype(BF16)
+            for k in range(nz)
+        ],
+        axis=0,
+    )
+    table = jnp.concatenate(
+        [fline[k] for k in range(nz)] + [jnp.zeros((128 - 4 * nz, devices), F32)], axis=0
+    )
+    sent = sum(
+        lax.dot_general(picked, part, (((1,), (1,)), ((), ())), preferred_element_type=F32)
+        for part in split3(table)
+    )
+    flane = lax.broadcasted_iota(I32, (devices, 128), 1)
+    frow = lax.broadcasted_iota(I32, (devices, 128), 0)
+    sent = jnp.where(lax.div(flane, 4) == lax.div(frow, plane), sent, 0.0)
+    fsend[...] = jnp.sum(sent.reshape(nz, plane, 128), axis=0).reshape(plane, 1, 128)
     for px, py in peers:
         pltpu.make_async_remote_copy(
             fsend.at[px * ny + py], frecv.at[q], fp_send, fp_recv, device_id=(px, py, z), device_id_type=MESH
-        ).start()
-    send_blocks(order[EARLY:LATE])
-    frecv[q] = fsend[q]
-    drain(frecv, plane - 1, fp_recv)
-    got = frecv[...].reshape(plane, 128)
-    group = lax.div(lax.broadcasted_iota(I32, (plane, 128), 1), 4)
-    source = lax.broadcasted_iota(I32, (plane, 128), 0)
-    for k in range(nz):
-        frelay[k] = jnp.sum(jnp.where(group == lax.rem(source + k, plane), got, 0.0), axis=0, keepdims=True)
-    farrived[z] = frelay[z]
-    for _, tz in lines:
-        pltpu.make_async_remote_copy(
-            frelay.at[tz], farrived.at[z], fz_send, fz_recv, device_id=(x, y, tz), device_id_type=MESH
         ).start()
     send_blocks(order[LATE:])
     owns = [
@@ -244,11 +251,10 @@
     place = jnp.concatenate(places, axis=1)
     picks = jnp.where(lax.broadcasted_iota(I32, (span, span), 0) == place, 1.0, 0.0).astype(BF16)
 
-    drain(farrived, nz - 1, fz_recv)
-    got = jnp.concatenate([farrived[k] for k in range(nz)], axis=0)
-    wide = jnp.broadcast_to(got[None], (plane, nz, 128)).reshape(devices, 128)
-    sender = lax.div(lax.broadcasted_iota(I32, (devices, 128), 0), nz)
-    fit = lax.div(flane, 4) == lax.rem(sender + z, plane)
+    frecv[q] = fsend[q]
+    drain(frecv, plane - 1, fp_recv)
+    wide = jnp.broadcast_to(frecv[...], (plane, nz, 128)).reshape(devices, 128)
+    fit = lax.div(flane, 4) == lax.rem(frow, nz)
     chosen = jnp.concatenate(
         [jnp.where(fit & (lax.rem(flane, 2) == level), wide, 0.0) for level in range(2)], axis=0
     )
@@ -280,7 +286,7 @@
     drain(cline, nz - 1, cz_send)
     drain(call, plane - 1, cp_send)
     drain(fsend, plane - 1, fp_send)
-    drain(farrived, nz - 1, fz_send)
+    drain(fline, nz - 1, fz_send)
     drain(arrived, devices - 2, b_send)
     pltpu.make_async_copy(acc, acc, near_send).wait()
 
@@ -335,12 +341,11 @@
                 pltpu.VMEM((span, 128), F32),
                 pltpu.VMEM((2, 2, span, 128), F32),
                 pltpu.VMEM((2, 2, span, 128), F32),
-                pltpu.VMEM((span, 128), F32),
                 pltpu.VMEM((2, 4 * devices, 128), F32),
                 pltpu.VMEM((plane, 1, 128), F32),
                 pltpu.VMEM((plane, 1, 128), F32),
-                pltpu.VMEM((nz, 1, 128), F32),
-                pltpu.VMEM((nz, 1, 128), F32),
+                pltpu.VMEM((1, 4, devices), F32),
+                pltpu.VMEM((nz, 4, devices), F32),
                 pltpu.VMEM((1, 1, 128), I32),
                 pltpu.VMEM((nz, 1, 128), I32),
                 pltpu.VMEM((1, 1, 128), I32),

time: 34.9 us -> 34.1 us (0.977)
  Pallas kernels: 34.2 us -> 33.3 us
    pallas_call x1, Pallas kernels: 32.9 us -> 32.1 us  [shards(): pl.pallas_call(functools.partial(kernel, sizes), out_shape=(jax.ShapeDtyp...]
where the time goes in v5:
time: 34.1 us; the launch traced here: 34 us
  Pallas kernels  33.3 us (98%)
  between operations  0.64 us (2%)
    pallas_call x1, Pallas kernels, shards(): pl.pallas_call(functools.partial(kernel, sizes), out_shape=(jax.ShapeDtyp...  32.1 us
    pallas_call x1, Pallas kernels, shards(): pl.pallas_call(put, out_shape=(jax.ShapeDtypeStruct((span, width), F32),...  1.24 us

profile of v5, /device:TPU:1, one launch (start us, length us, event | category | flops | bytes accessed | tf_op | source)
XLA Modules:
  0.0 34.0 jit_solution(9734715162969148941)
XLA Ops:
  0.6 32.1 %exchange.1 = (f32[256,4,128]{2,1,0:T(4,128)S(1)}, s32[8,512]{1,0:T(8,128)S(1)}) custom-call(f32[2048,256]{1,0:T(8,128)} %measures.1, s32[1,2048]{1,0:T(1,128)} %bitcast.6, s32[1,512]{1,0:T(1,128)} %keys_in.1), custom_call_target="tpu_custom_call" | custom-call | tf_op jit(solution)/shard_map/exchange/pallas_call | solution.py:328
  32.7 1.2 %put.1 = (f32[512,256]{1,0:T(8,128)}, s32[1,512]{1,0:T(1,128)}, s32[1,512]{1,0:T(1,128)}, s32[1,1]{1,0:T(1,128)}) custom-call(f32[1024,128]{1,0:T(8,128)S(1)} %bitcast.5, s32[8,512]{1,0:T(8,128)S(1)} %get-tuple-element.11.small), custom_call_target="tpu_custom_call" | custom-call | tf_op jit(solution)/shard_map/put/pallas_call | solution.py:365

commit v6 on v5

--- a/solution.py
+++ b/solution.py
@@ -181,7 +181,7 @@
 
     def hops(offset):
         i, j, side, k = offset
-        return min(i, nx - i) + min(j, ny - j) / 2 + (j % 2) * 0.1 + k
+        return 2 * (min(i, nx - i) + min(j, ny - j) / 2 + (j % 2) * 0.1) + k
 
     order = sorted(
         (

time: 34.1 us -> 34 us (level)
  no operation moved by 1% of the time
where the time goes in v6:
time: 34 us; the launch traced here: 33.8 us
  Pallas kernels  33.2 us (98%)
  between operations  0.64 us (2%)
    pallas_call x1, Pallas kernels, shards(): pl.pallas_call(functools.partial(kernel, sizes), out_shape=(jax.ShapeDtyp...  32 us
    pallas_call x1, Pallas kernels, shards(): pl.pallas_call(put, out_shape=(jax.ShapeDtypeStruct((span, width), F32),...  1.24 us

profile of v6, /device:TPU:1, one launch (start us, length us, event | category | flops | bytes accessed | tf_op | source)
XLA Modules:
  0.0 33.8 jit_solution(14871027608612458011)
XLA Ops:
  0.6 32.0 %exchange.1 = (f32[256,4,128]{2,1,0:T(4,128)S(1)}, s32[8,512]{1,0:T(8,128)S(1)}) custom-call(f32[2048,256]{1,0:T(8,128)} %measures.1, s32[1,2048]{1,0:T(1,128)} %bitcast.6, s32[1,512]{1,0:T(1,128)} %keys_in.1), custom_call_target="tpu_custom_call" | custom-call | tf_op jit(solution)/shard_map/exchange/pallas_call | solution.py:328
  32.6 1.2 %put.1 = (f32[512,256]{1,0:T(8,128)}, s32[1,512]{1,0:T(1,128)}, s32[1,512]{1,0:T(1,128)}, s32[1,1]{1,0:T(1,128)}) custom-call(f32[1024,128]{1,0:T(8,128)S(1)} %bitcast.5, s32[8,512]{1,0:T(8,128)S(1)} %get-tuple-element.11.small), custom_call_target="tpu_custom_call" | custom-call | tf_op jit(solution)/shard_map/put/pallas_call | solution.py:365

commit v7 on v6

--- a/solution.py
+++ b/solution.py
@@ -10,7 +10,7 @@
 AXES = ("gx", "gy", "gz")
 MESH = pl.DeviceIdType.MESH
 F32, BF16, I32 = jnp.float32, jnp.bfloat16, jnp.int32
-CHUNKS = 4
+CHUNKS = 2
 LATE = 150
 
 
@@ -65,10 +65,10 @@
     peers = [(xs[i], ys[j]) for i, j in across]
 
     barrier = pltpu.get_barrier_semaphore()
-    for px, py in peers:
-        pl.semaphore_signal(barrier, inc=1, device_id=(px, py, z), device_id_type=MESH)
-    for _, tz in lines:
-        pl.semaphore_signal(barrier, inc=1, device_id=(x, y, tz), device_id_type=MESH)
+    greeted = [(min(i, nx - i) + min(j, ny - j) / 2, (px, py, z)) for (i, j), (px, py) in zip(across, peers)]
+    greeted += [(min(k, nz - k), (x, y, tz)) for k, tz in lines]
+    for _, place in sorted(greeted, key=lambda t: -t[0]):
+        pl.semaphore_signal(barrier, inc=1, device_id=place, device_id_type=MESH)
 
     loads = [
         pltpu.make_async_copy(

time: 34 us -> 33.7 us (level)
  no operation moved by 1% of the time
where the time goes in v7:
time: 33.7 us; the launch traced here: 33.6 us
  Pallas kernels  32.9 us (98%)
  between operations  0.64 us (2%)
    pallas_call x1, Pallas kernels, shards(): pl.pallas_call(functools.partial(kernel, sizes), out_shape=(jax.ShapeDtyp...  31.7 us
    pallas_call x1, Pallas kernels, shards(): pl.pallas_call(put, out_shape=(jax.ShapeDtypeStruct((span, width), F32),...  1.24 us

profile of v7, /device:TPU:1, one launch (start us, length us, event | category | flops | bytes accessed | tf_op | source)
XLA Modules:
  0.0 33.6 jit_solution(9690127082110995072)
XLA Ops:
  0.6 31.7 %exchange.1 = (f32[256,4,128]{2,1,0:T(4,128)S(1)}, s32[8,512]{1,0:T(8,128)S(1)}) custom-call(f32[2048,256]{1,0:T(8,128)} %measures.1, s32[1,2048]{1,0:T(1,128)} %bitcast.6, s32[1,512]{1,0:T(1,128)} %keys_in.1), custom_call_target="tpu_custom_call" | custom-call | tf_op jit(solution)/shard_map/exchange/pallas_call | solution.py:328
  32.3 1.2 %put.1 = (f32[512,256]{1,0:T(8,128)}, s32[1,512]{1,0:T(1,128)}, s32[1,512]{1,0:T(1,128)}, s32[1,1]{1,0:T(1,128)}) custom-call(f32[1024,128]{1,0:T(8,128)S(1)} %bitcast.5, s32[8,512]{1,0:T(8,128)S(1)} %get-tuple-element.11.small), custom_call_target="tpu_custom_call" | custom-call | tf_op jit(solution)/shard_map/put/pallas_call | solution.py:365

commit v8 on v7

--- a/solution.py
+++ b/solution.py
@@ -11,6 +11,7 @@
 MESH = pl.DeviceIdType.MESH
 F32, BF16, I32 = jnp.float32, jnp.bfloat16, jnp.int32
 CHUNKS = 2
+FRONT = 1280
 LATE = 150
 
 
@@ -43,7 +44,7 @@
     nx, ny, nz = sizes
     plane, devices = nx * ny, nx * ny * nz
     rows = measures.shape[0]
-    step = rows // CHUNKS
+    bounds = ((0, FRONT), (FRONT, rows))
     span = 2 * devices
     x, y, z = (lax.axis_index(a) for a in AXES)
     q = x * ny + y
@@ -72,9 +73,9 @@
 
     loads = [
         pltpu.make_async_copy(
-            measures.at[pl.ds(c * step, step)], values.at[pl.ds(c * step, step)], load_sems.at[c]
+            measures.at[pl.ds(low, high - low)], values.at[pl.ds(low, high - low)], load_sems.at[c]
         )
-        for c in range(CHUNKS)
+        for c, (low, high) in enumerate(bounds)
     ]
     inputs = [
         pltpu.make_async_copy(src, dst, load_sems.at[CHUNKS + i])
@@ -91,14 +92,15 @@
     crow[0] = mine
     cline[z] = mine
 
-    labels = lax.broadcasted_iota(I32, (span, step), 0)
-
-    ones = jnp.ones((step, 128), BF16)
 
     def accumulate(c):
+        low, high = bounds[c]
+        step = high - low
+        labels = lax.broadcasted_iota(I32, (span, step), 0)
+        ones = jnp.ones((step, 128), BF16)
         loads[c].wait()
-        hits = jnp.where(labels == index[0:1, c * step : (c + 1) * step], 1.0, 0.0).astype(BF16)
-        hi, lo = split2(values[pl.ds(c * step, step)])
+        hits = jnp.where(labels == index[0:1, low:high], 1.0, 0.0).astype(BF16)
+        hi, lo = split2(values[pl.ds(low, step)])
         part = dot(hits, hi) + dot(hits, lo)
         seen = dot(hits, ones)
         if c == 0:

time: 33.7 us -> 33.6 us (level)
  no operation moved by 1% of the time
where the time goes in v8:
time: 33.6 us; the launch traced here: 33.5 us
  Pallas kernels  32.8 us (98%)
  between operations  0.64 us (2%)
    pallas_call x1, Pallas kernels, shards(): pl.pallas_call(functools.partial(kernel, sizes), out_shape=(jax.ShapeDtyp...  31.6 us
    pallas_call x1, Pallas kernels, shards(): pl.pallas_call(put, out_shape=(jax.ShapeDtypeStruct((span, width), F32),...  1.24 us

profile of v8, /device:TPU:1, one launch (start us, length us, event | category | flops | bytes accessed | tf_op | source)
XLA Modules:
  0.0 33.5 jit_solution(4583112650864959634)
XLA Ops:
  0.6 31.6 %exchange.1 = (f32[256,4,128]{2,1,0:T(4,128)S(1)}, s32[8,512]{1,0:T(8,128)S(1)}) custom-call(f32[2048,256]{1,0:T(8,128)} %measures.1, s32[1,2048]{1,0:T(1,128)} %bitcast.6, s32[1,512]{1,0:T(1,128)} %keys_in.1), custom_call_target="tpu_custom_call" | custom-call | tf_op jit(solution)/shard_map/exchange/pallas_call | solution.py:330
  32.2 1.2 %put.1 = (f32[512,256]{1,0:T(8,128)}, s32[1,512]{1,0:T(1,128)}, s32[1,512]{1,0:T(1,128)}, s32[1,1]{1,0:T(1,128)}) custom-call(f32[1024,128]{1,0:T(8,128)S(1)} %bitcast.5, s32[8,512]{1,0:T(8,128)S(1)} %get-tuple-element.11.small), custom_call_target="tpu_custom_call" | custom-call | tf_op jit(solution)/shard_map/put/pallas_call | solution.py:367
